TPU v7x, 32 devices: a whole 2x2x4 slice. The times are simulated.
32 devices in a mesh: row: 4 (over y, x), col: 4 (over z), depth: 2 (over core).
Axes of the slice: x: 2, y: 2, z: 4, core: 2. Of those that a mesh axis runs over, the one named last changes fastest.
Arguments:
- layers: float32 [2, 4096, 4096], P('depth', 'row', 'col'), may hold values from -3 to 134.2, as said below
Outputs:
- factor: float32 [2, 4096, 512], P(None, 'row', 'depth')
- schur: float32 [4096, 4096], P(('row', 'depth'), 'col')
Inputs may be any that keep to these rules, and one draw needn't show every extreme that they name: Read in matrix order, each layer is symmetric, and the sum over layers is symmetric positive definite with a diagonal of order sqrt(4096).
All inputs are finite; a program needn't handle non-finite values.
Results may differ from a plain program's by a relative error of at most 0.0001.
Values sent between devices are 32-bit elements; how exact they have to be, the bound alone decides.
A program may use at most 192 MiB of HBM per device.

v0:
```python
import jax
import jax.numpy as jnp
from jax import lax
from jax.sharding import PartitionSpec as P

PANEL = 512
PANELS = 2


def broadcast(value, axis, source):
    kept = jnp.where(lax.axis_index(axis) == source, value, 0).astype(value.dtype)
    return lax.psum(kept, axis)


def block_inverse(diagonal, identity_block):
    lower_diag = jnp.linalg.cholesky(diagonal)
    return jax.scipy.linalg.solve_triangular(lower_diag, identity_block, lower=True)


def outer_update(left_rows, right_rows):
    return lax.dot_general(
        left_rows,
        right_rows,
        (((1,), (1,)), ((), ())),
        precision=lax.Precision.HIGHEST,
        preferred_element_type=jnp.float32,
    )


def per_device(layers):
    row_groups = lax.axis_size("row")
    col_groups = lax.axis_size("col")
    depth_groups = lax.axis_size("depth")
    row_index = lax.axis_index("row")
    col_index = lax.axis_index("col")
    depth_index = lax.axis_index("depth")
    layer_part = layers[0]
    rows_local = layer_part.shape[0]
    cols_local = layer_part.shape[1]
    slice_width = PANEL // depth_groups
    quarter_rows = rows_local // depth_groups
    local_blocks = rows_local // PANEL
    row_block = jnp.arange(rows_local, dtype=jnp.int32) // PANEL * row_groups + row_index
    col_block = jnp.arange(cols_local, dtype=jnp.int32) // PANEL * col_groups + col_index
    identity_block = jnp.eye(PANEL, dtype=jnp.float32)
    factor_list = []
    schur = None
    for panel_step in range(PANELS):
        owner_col = panel_step % col_groups
        local_col = panel_step // col_groups
        owner_row = panel_step % row_groups
        local_row = panel_step // row_groups
        column = layer_part[:, local_col * PANEL : (local_col + 1) * PANEL]
        layer_diag = broadcast(
            column[local_row * PANEL : (local_row + 1) * PANEL], "row", owner_row
        )
        diagonal = lax.psum(layer_diag, "depth")
        quarter = lax.psum_scatter(column, "depth", scatter_dimension=0, tiled=True)
        inverse = block_inverse(diagonal, identity_block)
        solved = jnp.dot(quarter, inverse.T, precision=lax.Precision.HIGHEST)
        quarter_block = lax.dynamic_slice_in_dim(
            row_block, depth_index * quarter_rows, quarter_rows, 0
        )
        solved = jnp.where(quarter_block[:, None] >= panel_step, solved, 0.0)
        row_slice = lax.all_to_all(solved, "depth", split_axis=1, concat_axis=0, tiled=True)
        panel_rows = broadcast(row_slice, "col", owner_col)
        factor_list.append(panel_rows)
        update_rows = jnp.where(row_block[:, None] > panel_step, panel_rows, 0.0)
        gathered = lax.all_gather(panel_rows, "row", axis=0, tiled=True)
        grouped = gathered.reshape(
            row_groups // col_groups, col_groups, local_blocks, PANEL, slice_width
        )
        picked = lax.dynamic_index_in_dim(grouped, col_index, 1, keepdims=False)
        column_rows = picked.transpose(1, 0, 2, 3).reshape(cols_local, slice_width)
        update_cols = jnp.where(col_block[:, None] > panel_step, column_rows, 0.0)
        if panel_step + 1 < PANELS:
            layer_part = layer_part - outer_update(update_rows, update_cols)
        else:
            schur = lax.psum_scatter(
                layer_part - outer_update(update_rows, update_cols),
                "depth",
                scatter_dimension=0,
                tiled=True,
            )
    return (jnp.stack(factor_list), schur)


def solution(mesh):
    return jax.shard_map(
        per_device,
        mesh=mesh,
        in_specs=(P("depth", "row", "col"),),
        out_specs=(P(None, "row", "depth"), P(("row", "depth"), "col")),
        check_vma=False,
    )
```

profile of v0, /device:TPU:0, one launch (start us, length us, event | category | flops | bytes accessed | tf_op | source)
XLA Modules:
  0.0 728.1 jit_solution(16254621082217000149)
XLA Ops:
  7.2 5.4 copy.3
  14.9 55.3 %all-reduce.8.cloned.1.call-done = f32[512,512]{0,1:T(8,128)} async-done(((f32[512,512]{0,1:T(8,128)}), f32[512,512]{0,1:T(8,128)}) %all-reduce.8.cloned.1.call-update) | async-done | bytes 1048592 | tf_op jit(solution)/shard_map/psum | solution.py:12
  73.8 18.3 %all-reduce.10.cloned.1.call-done = f32[512,512]{0,1:T(8,128)} async-done(((f32[512,512]{0,1:T(8,128)}), f32[512,512]{0,1:T(8,128)}) %all-reduce.10.cloned.1.call-update) | async-done | bytes 1048592 | tf_op jit(solution)/shard_map/psum | solution.py:57
  95.1 11.7 %cholesky.286 = f32[128,128]{1,0:T(8,128)S(1)} custom-call(f32[128,128]{1,0:T(8,128)S(1)} %cholesky.426), custom_call_target="Cholesky" | custom-call | tf_op jit(solution)/shard_map/jit(cholesky)/cholesky | solution.py:16
  106.8 9.8 %custom-call.27 = f32[1,128,128]{1,2,0:T(8,128)S(1)} custom-call(f32[1,128,128]{2,1,0:T(8,128)S(1)} %get-tuple-element.61), custom_call_target="InvertDiagBlocksLowerTriangular" | custom-call | tf_op jit(solution)/shard_map/jit(cholesky)/cholesky | solution.py:16
  117.4 11.7 %cholesky.305 = f32[128,128]{1,0:T(8,128)S(1)} custom-call(f32[128,128]{1,0:T(8,128)S(1)} %cholesky.430), custom_call_target="Cholesky" | custom-call | tf_op jit(solution)/shard_map/jit(cholesky)/cholesky | solution.py:16
  129.2 10.0 %custom-call.28 = f32[1,128,128]{1,2,0:T(8,128)S(1)} custom-call(f32[1,128,128]{2,1,0:T(8,128)S(1)} %get-tuple-element.58), custom_call_target="InvertDiagBlocksLowerTriangular" | custom-call | tf_op jit(solution)/shard_map/jit(cholesky)/cholesky | solution.py:16
  139.8 11.7 %cholesky.326 = f32[128,128]{1,0:T(8,128)S(1)} custom-call(f32[128,128]{1,0:T(8,128)S(1)} %cholesky.435), custom_call_target="Cholesky" | custom-call | tf_op jit(solution)/shard_map/jit(cholesky)/cholesky | solution.py:16
  151.6 9.8 %custom-call.29 = f32[1,128,128]{1,2,0:T(8,128)S(1)} custom-call(f32[1,128,128]{2,1,0:T(8,128)S(1)} %get-tuple-element.55), custom_call_target="InvertDiagBlocksLowerTriangular" | custom-call | tf_op jit(solution)/shard_map/jit(cholesky)/cholesky | solution.py:16
  162.0 11.7 %cholesky.343 = f32[128,128]{1,0:T(8,128)S(1)} custom-call(f32[128,128]{1,0:T(8,128)S(1)} %convolution_subtract_fusion.13), custom_call_target="Cholesky" | custom-call | tf_op jit(solution)/shard_map/jit(cholesky)/cholesky | solution.py:16
  178.9 8.1 %while.4 = (s32[]{:T(128)}, f32[512,512]{1,0:T(8,128)S(1)}, s32[4,2]{0,1:T(2,128)S(1)}, f32[4,128,128]{2,1,0:T(8,128)S(1)}, s32[]{:T(128)}) while((s32[]{:T(128)}, f32[512,512]{1,0:T(8,128)S(1)}, s32[4,2]{0,1:T(2,128)S(1)}, f32[4,128,128]{2,1,0:T(8,128)S(1)}, s32[]{:T(128)}) %tuple.57), condition=%wide.while_cond, body=%wide.while_body.sunk | while | flops 2 | bytes 131181 | solution.py:17
  187.0 39.3 %custom-call.30 = f32[4,128,128]{1,2,0:T(8,128)S(1)} custom-call(f32[4,128,128]{2,1,0:T(8,128)S(1)} %get-tuple-element.18), custom_call_target="InvertDiagBlocksLowerTriangular" | custom-call | tf_op jit(solution)/shard_map/jit(_solve_triangular)/triangular_solve | solution.py:17
  234.8 5.7 all_to_all.26
  242.0 53.2 %all-reduce.12.cloned.1.call-done = f32[1024,256]{1,0:T(8,128)} async-done(((f32[1024,256]{1,0:T(8,128)}), f32[1024,256]{1,0:T(8,128)}) %all-reduce.12.cloned.1.call-update) | async-done | bytes 1048592 | tf_op jit(solution)/shard_map/psum | solution.py:12
  295.3 53.5 %all-gather.3.cloned.1.call-done = f32[4096,256]{1,0:T(8,128)} async-done(((f32[1024,256]{1,0:T(8,128)}), f32[4096,256]{1,0:T(8,128)}) %all-gather.3.cloned.1.call-update) | async-done | bytes 4194320 | tf_op jit(solution)/shard_map/all_gather | solution.py:69
  351.2 3.9 convolution_subtract_fusion.1
  358.2 52.6 %all-reduce.14.cloned.1.call-done = f32[512,512]{0,1:T(8,128)} async-done(((f32[512,512]{0,1:T(8,128)}), f32[512,512]{0,1:T(8,128)}) %all-reduce.14.cloned.1.call-update) | async-done | bytes 1048592 | tf_op jit(solution)/shard_map/psum | solution.py:12
  414.2 18.3 %all-reduce.16.cloned.1.call-done = f32[512,512]{0,1:T(8,128)} async-done(((f32[512,512]{0,1:T(8,128)}), f32[512,512]{0,1:T(8,128)}) %all-reduce.16.cloned.1.call-update) | async-done | bytes 1048592 | tf_op jit(solution)/shard_map/psum | solution.py:57
  436.5 11.7 %cholesky.358 = f32[128,128]{1,0:T(8,128)S(1)} custom-call(f32[128,128]{1,0:T(8,128)S(1)} %cholesky.439), custom_call_target="Cholesky" | custom-call | tf_op jit(solution)/shard_map/jit(cholesky)/cholesky | solution.py:16
  448.4 9.8 %custom-call.31 = f32[1,128,128]{1,2,0:T(8,128)S(1)} custom-call(f32[1,128,128]{2,1,0:T(8,128)S(1)} %get-tuple-element.51), custom_call_target="InvertDiagBlocksLowerTriangular" | custom-call | tf_op jit(solution)/shard_map/jit(cholesky)/cholesky | solution.py:16
  460.7 11.7 %cholesky.377 = f32[128,128]{1,0:T(8,128)S(1)} custom-call(f32[128,128]{1,0:T(8,128)S(1)} %cholesky.443), custom_call_target="Cholesky" | custom-call | tf_op jit(solution)/shard_map/jit(cholesky)/cholesky | solution.py:16
  472.5 10.0 %custom-call.32 = f32[1,128,128]{1,2,0:T(8,128)S(1)} custom-call(f32[1,128,128]{2,1,0:T(8,128)S(1)} %get-tuple-element.48), custom_call_target="InvertDiagBlocksLowerTriangular" | custom-call | tf_op jit(solution)/shard_map/jit(cholesky)/cholesky | solution.py:16
  484.1 11.7 %cholesky.398 = f32[128,128]{1,0:T(8,128)S(1)} custom-call(f32[128,128]{1,0:T(8,128)S(1)} %cholesky.448), custom_call_target="Cholesky" | custom-call | tf_op jit(solution)/shard_map/jit(cholesky)/cholesky | solution.py:16
  495.8 9.8 %custom-call.33 = f32[1,128,128]{1,2,0:T(8,128)S(1)} custom-call(f32[1,128,128]{2,1,0:T(8,128)S(1)} %get-tuple-element.45), custom_call_target="InvertDiagBlocksLowerTriangular" | custom-call | tf_op jit(solution)/shard_map/jit(cholesky)/cholesky | solution.py:16
  507.1 11.7 %cholesky.415 = f32[128,128]{1,0:T(8,128)S(1)} custom-call(f32[128,128]{1,0:T(8,128)S(1)} %convolution_subtract_fusion.12), custom_call_target="Cholesky" | custom-call | tf_op jit(solution)/shard_map/jit(cholesky)/cholesky | solution.py:16
  525.3 11.7 %while.5 = (s32[]{:T(128)}, f32[512,512]{1,0:T(8,128)}, s32[4,2]{0,1:T(2,128)S(1)}, f32[4,128,128]{2,1,0:T(8,128)S(1)}, s32[]{:T(128)}) while((s32[]{:T(128)}, f32[512,512]{1,0:T(8,128)}, s32[4,2]{0,1:T(2,128)S(1)}, f32[4,128,128]{2,1,0:T(8,128)S(1)}, s32[]{:T(128)}) %tuple.85), condition=%wide.while_cond.clone, body=%wide.while_body.clone.sunk | while | flops 2 | bytes 131181 | solution.py:17
  537.1 39.3 %custom-call.34 = f32[4,128,128]{1,2,0:T(8,128)S(1)} custom-call(f32[4,128,128]{2,1,0:T(8,128)S(1)} %get-tuple-element.19), custom_call_target="InvertDiagBlocksLowerTriangular" | custom-call | tf_op jit(solution)/shard_map/jit(_solve_triangular)/triangular_solve | solution.py:17
  585.3 4.6 all_to_all.27
  591.4 53.2 %all-reduce.18.cloned.1.call-done = f32[1024,256]{1,0:T(8,128)} async-done(((f32[1024,256]{1,0:T(8,128)}), f32[1024,256]{1,0:T(8,128)}) %all-reduce.18.cloned.1.call-update) | async-done | bytes 1048592 | tf_op jit(solution)/shard_map/psum | solution.py:12
  644.7 53.5 %all-gather.5.cloned.1.call-done = f32[4096,256]{1,0:T(8,128)} async-done(((f32[1024,256]{1,0:T(8,128)}), f32[4096,256]{1,0:T(8,128)}) %all-gather.5.cloned.1.call-update) | async-done | bytes 4194320 | tf_op jit(solution)/shard_map/all_gather | solution.py:69
  700.6 5.5 convolution_subtract_fusion
  707.6 10.6 %reduce-scatter.8.cloned.1.call-done = f32[512,1024]{0,1:T(8,128)} async-done(((f32[1024,1024]{0,1:T(8,128)}), f32[512,1024]{0,1:T(8,128)}) %reduce-scatter.8.cloned.1.call-update) | async-done | bytes 2097168 | tf_op jit(solution)/shard_map/reduce_scatter | solution.py:79
  (145 shorter events, 83.1 us)
Async XLA Ops:
  7.2 63.1 %all-reduce.8.cloned.1.call-start = ((), (), s32[]{:S(2)}) async-start(), calls=%async_computation.5 | async-start | bytes 2097152 | tf_op jit(solution)/shard_map/psum | solution.py:12
  14.9 77.1 %all-reduce.10.cloned.1.call-start = ((), (), s32[]{:S(2)}) async-start(), calls=%async_computation.6 | async-start | bytes 2097152 | tf_op jit(solution)/shard_map/psum | solution.py:57
  70.3 160.1 %reduce-scatter.4.cloned.1.call-start = ((), (), s32[]{:S(2)}) async-start(), calls=%async_computation.7 | async-start | bytes 3145728 | tf_op jit(solution)/shard_map/reduce_scatter | solution.py:58
  73.5 221.7 %all-reduce.12.cloned.1.call-start = ((), (), s32[]{:S(2)}) async-start(), calls=%async_computation.8 | async-start | bytes 2097152 | tf_op jit(solution)/shard_map/psum | solution.py:12
  226.4 2.1 copy-start.6
  241.9 106.8 %all-gather.3.cloned.1.call-start = ((), (), s32[]{:S(2)}) async-start(), calls=%async_computation.9 | async-start | bytes 5242880 | tf_op jit(solution)/shard_map/all_gather | solution.py:69
  295.2 55.2 %copy-start.3 = (f32[1024,256]{1,0:T(8,128)S(1)}, f32[1024,256]{1,0:T(8,128)}, u32[]{:S(2)}) copy-start(f32[1024,256]{1,0:T(8,128)} %all-reduce.12.cloned.1.call-done) | copy-start | bytes 3145732
  295.2 115.5 %all-reduce.14.cloned.1.call-start = ((), (), s32[]{:S(2)}) async-start(), calls=%async_computation.11 | async-start | bytes 2097152 | tf_op jit(solution)/shard_map/psum | solution.py:12
  348.7 2.5 copy-start
  355.1 1.9 copy-start.1
  358.1 74.4 %all-reduce.16.cloned.1.call-start = ((), (), s32[]{:S(2)}) async-start(), calls=%async_computation.12 | async-start | bytes 2097152 | tf_op jit(solution)/shard_map/psum | solution.py:57
  410.8 171.5 %reduce-scatter.6.cloned.1.call-start = ((), (), s32[]{:S(2)}) async-start(), calls=%async_computation.10 | async-start | bytes 3145728 | tf_op jit(solution)/shard_map/reduce_scatter | solution.py:58
  414.0 230.6 %all-reduce.18.cloned.1.call-start = ((), (), s32[]{:S(2)}) async-start(), calls=%async_computation.13 | async-start | bytes 2097152 | tf_op jit(solution)/shard_map/psum | solution.py:12
  435.5 1.0 copy-start.5
  591.4 106.8 %all-gather.5.cloned.1.call-start = ((), (), s32[]{:S(2)}) async-start(), calls=%async_computation.14 | async-start | bytes 5242880 | tf_op jit(solution)/shard_map/all_gather | solution.py:69
  644.6 55.2 %copy-start.4 = (f32[1024,256]{1,0:T(8,128)S(1)}, f32[1024,256]{1,0:T(8,128)}, u32[]{:S(2)}) copy-start(f32[1024,256]{1,0:T(8,128)} %all-reduce.18.cloned.1.call-done) | copy-start | bytes 3145732
  644.6 73.6 %reduce-scatter.8.cloned.1.call-start = ((), (), s32[]{:S(2)}) async-start(), calls=%async_computation.15 | async-start | bytes 6291456 | tf_op jit(solution)/shard_map/reduce_scatter | solution.py:79
  698.1 2.5 copy-start.2
Sparse Core Ops, SparseCore 0:
  15.0 55.1 all-reduce.7
  72.6 19.4 all-reduce.9
  94.8 10.8 reduce-scatter.3
  242.0 53.0 all-reduce.11
  296.8 51.8 all-gather.2
  358.2 52.4 all-reduce.13
  413.1 19.4 all-reduce.15
  435.3 10.7 reduce-scatter.5
  591.5 53.0 all-reduce.17
  646.3 51.8 all-gather.4
  706.3 11.8 reduce-scatter.7
where the time goes:
time: 738 us; the launch traced here: 728 us
  waiting for transfers between devices  369 us (50%)
  other arithmetic  247 us (33%)
  local copies, waits for them, and re-layouts  49.1 us (7%)
  matrix products  32.6 us (4%)
  between operations  20 us (3%)
  blocking collectives  10.3 us (1%)
    psum x4, waiting for transfers between devices, broadcast(): return lax.psum(kept, axis)  214 us
    another operation x29, other arithmetic, block_inverse(): lower_diag = jnp.linalg.cholesky(diagonal)  158 us
    all_gather x2, waiting for transfers between devices, per_device(): gathered = lax.all_gather(panel_rows, 'row', axis=0, tiled=True)  107 us
    another operation x5, other arithmetic, block_inverse(): jax.scipy.linalg.solve_triangular(lower_diag, identity_block, lower=True)  80.1 us
    psum x2, waiting for transfers between devices, per_device(): diagonal = lax.psum(layer_diag, 'depth')  36.6 us
    another operation x27, local copies, waits for them, and re-layouts, block_inverse(): jax.scipy.linalg.solve_triangular(lower_diag, identity_block, lower=True)  19.7 us
  transfers between devices with their start and end apart: 11, of which 9 were waited for; matrix products, arithmetic and copies ran while one was open for 40% of the time, Pallas kernels for 0%

commit v1 on v0

--- a/solution.py
+++ b/solution.py
@@ -54,7 +54,7 @@
         layer_diag = broadcast(
             column[local_row * PANEL : (local_row + 1) * PANEL], "row", owner_row
         )
-        diagonal = lax.psum(layer_diag, "depth")
+        diagonal = jnp.sum(lax.all_gather(layer_diag, "depth"), axis=0)
         quarter = lax.psum_scatter(column, "depth", scatter_dimension=0, tiled=True)
         inverse = block_inverse(diagonal, identity_block)
         solved = jnp.dot(quarter, inverse.T, precision=lax.Precision.HIGHEST)

time: 738 us -> 714 us (0.967)
  waiting for transfers between devices: 369 us -> 351 us
  local copies, waits for them, and re-layouts: 49.1 us -> 38.7 us
    psum x2 -> x0, waiting for transfers between devices: 36.6 us -> none  [per_device(): diagonal = lax.psum(layer_diag, 'depth')]
    all_gather x0 -> x2, waiting for transfers between devices: none -> 17.4 us  [per_device(): diagonal = jnp.sum(lax.all_gather(layer_diag, 'depth'), axis=0)]
  transfers between devices with their start and end apart: 11 -> 11, of which waited for: 9 -> 9; matrix products, arithmetic and copies ran while one was open for 40% -> 42% of each run, Pallas kernels for 0% -> 0%
where the time goes in v1:
time: 714 us; the launch traced here: 704 us
  waiting for transfers between devices  351 us (49%)
  other arithmetic  249 us (35%)
  local copies, waits for them, and re-layouts  38.7 us (5%)
  matrix products  35 us (5%)
  between operations  19.8 us (3%)
  blocking collectives  9.15 us (1%)
    psum x4, waiting for transfers between devices, broadcast(): return lax.psum(kept, axis)  216 us
    another operation x29, other arithmetic, block_inverse(): lower_diag = jnp.linalg.cholesky(diagonal)  158 us
    all_gather x2, waiting for transfers between devices, per_device(): gathered = lax.all_gather(panel_rows, 'row', axis=0, tiled=True)  107 us
    another operation x5, other arithmetic, block_inverse(): jax.scipy.linalg.solve_triangular(lower_diag, identity_block, lower=True)  79.9 us
    another operation x27, local copies, waits for them, and re-layouts, block_inverse(): jax.scipy.linalg.solve_triangular(lower_diag, identity_block, lower=True)  19.2 us
    all_gather x2, waiting for transfers between devices, per_device(): diagonal = jnp.sum(lax.all_gather(layer_diag, 'depth'), axis=0)  17.4 us
  transfers between devices with their start and end apart: 11, of which 9 were waited for; matrix products, arithmetic and copies ran while one was open for 42% of the time, Pallas kernels for 0%

profile of v1, /device:TPU:0, one launch (start us, length us, event | category | flops | bytes accessed | tf_op | source)
XLA Modules:
  0.0 704.3 jit_solution(365314277607581835)
XLA Ops:
  9.6 57.3 %all-reduce.6.cloned.1.call-done = f32[1,512,512]{2,1,0:T(8,128)} async-done(((f32[1,512,512]{2,1,0:T(8,128)}), f32[1,512,512]{2,1,0:T(8,128)}) %all-reduce.6.cloned.1.call-update) | async-done | bytes 1048592 | tf_op jit(solution)/shard_map/psum | solution.py:12
  70.3 8.7 %all-gather.5.cloned.1.call-done = f32[2,512,512]{2,1,0:T(8,128)} async-done(((f32[1,512,512]{2,1,0:T(8,128)}), f32[2,512,512]{2,1,0:T(8,128)}) %all-gather.5.cloned.1.call-update) | async-done | bytes 2097168 | tf_op jit(solution)/shard_map/all_gather | solution.py:57
  82.4 11.7 %cholesky.286 = f32[128,128]{1,0:T(8,128)S(1)} custom-call(f32[128,128]{1,0:T(8,128)S(1)} %cholesky.426), custom_call_target="Cholesky" | custom-call | tf_op jit(solution)/shard_map/jit(cholesky)/cholesky | solution.py:16
  94.2 9.8 %custom-call.27 = f32[1,128,128]{1,2,0:T(8,128)S(1)} custom-call(f32[1,128,128]{2,1,0:T(8,128)S(1)} %get-tuple-element.59), custom_call_target="InvertDiagBlocksLowerTriangular" | custom-call | tf_op jit(solution)/shard_map/jit(cholesky)/cholesky | solution.py:16
  106.6 11.7 %cholesky.305 = f32[128,128]{1,0:T(8,128)S(1)} custom-call(f32[128,128]{1,0:T(8,128)S(1)} %cholesky.430), custom_call_target="Cholesky" | custom-call | tf_op jit(solution)/shard_map/jit(cholesky)/cholesky | solution.py:16
  118.4 10.2 %custom-call.28 = f32[1,128,128]{1,2,0:T(8,128)S(1)} custom-call(f32[1,128,128]{2,1,0:T(8,128)S(1)} %get-tuple-element.56), custom_call_target="InvertDiagBlocksLowerTriangular" | custom-call | tf_op jit(solution)/shard_map/jit(cholesky)/cholesky | solution.py:16
  130.2 11.7 %cholesky.326 = f32[128,128]{1,0:T(8,128)S(1)} custom-call(f32[128,128]{1,0:T(8,128)S(1)} %cholesky.435), custom_call_target="Cholesky" | custom-call | tf_op jit(solution)/shard_map/jit(cholesky)/cholesky | solution.py:16
  142.0 9.8 %custom-call.29 = f32[1,128,128]{1,2,0:T(8,128)S(1)} custom-call(f32[1,128,128]{2,1,0:T(8,128)S(1)} %get-tuple-element.53), custom_call_target="InvertDiagBlocksLowerTriangular" | custom-call | tf_op jit(solution)/shard_map/jit(cholesky)/cholesky | solution.py:16
  153.2 11.9 %cholesky.343 = f32[128,128]{1,0:T(8,128)S(1)} custom-call(f32[128,128]{1,0:T(8,128)S(1)} %convolution_subtract_fusion.13), custom_call_target="Cholesky" | custom-call | tf_op jit(solution)/shard_map/jit(cholesky)/cholesky | solution.py:16
  169.7 7.6 %while.4 = (s32[]{:T(128)}, f32[512,512]{1,0:T(8,128)S(1)}, s32[4,2]{0,1:T(2,128)S(1)}, f32[4,128,128]{2,1,0:T(8,128)S(1)}, s32[]{:T(128)}) while((s32[]{:T(128)}, f32[512,512]{1,0:T(8,128)S(1)}, s32[4,2]{0,1:T(2,128)S(1)}, f32[4,128,128]{2,1,0:T(8,128)S(1)}, s32[]{:T(128)}) %tuple.56), condition=%wide.while_cond, body=%wide.while_body.sunk | while | flops 2 | bytes 131181 | solution.py:17
  177.3 39.3 %custom-call.30 = f32[4,128,128]{1,2,0:T(8,128)S(1)} custom-call(f32[4,128,128]{2,1,0:T(8,128)S(1)} %get-tuple-element.18), custom_call_target="InvertDiagBlocksLowerTriangular" | custom-call | tf_op jit(solution)/shard_map/jit(_solve_triangular)/triangular_solve | solution.py:17
  222.9 4.6 all_to_all.26
  229.0 53.2 %all-reduce.8.cloned.1.call-done = f32[1024,256]{1,0:T(8,128)} async-done(((f32[1024,256]{1,0:T(8,128)}), f32[1024,256]{1,0:T(8,128)}) %all-reduce.8.cloned.1.call-update) | async-done | bytes 1048592 | tf_op jit(solution)/shard_map/psum | solution.py:12
  282.2 53.5 %all-gather.7.cloned.1.call-done = f32[4096,256]{1,0:T(8,128)} async-done(((f32[1024,256]{1,0:T(8,128)}), f32[4096,256]{1,0:T(8,128)}) %all-gather.7.cloned.1.call-update) | async-done | bytes 4194320 | tf_op jit(solution)/shard_map/all_gather | solution.py:69
  338.2 3.8 convolution_subtract_fusion.1
  345.1 52.6 %all-reduce.10.cloned.1.call-done = f32[1,512,512]{2,1,0:T(8,128)} async-done(((f32[1,512,512]{2,1,0:T(8,128)}), f32[1,512,512]{2,1,0:T(8,128)}) %all-reduce.10.cloned.1.call-update) | async-done | bytes 1048592 | tf_op jit(solution)/shard_map/psum | solution.py:12
  401.1 8.7 %all-gather.9.cloned.1.call-done = f32[2,512,512]{2,1,0:T(8,128)} async-done(((f32[1,512,512]{2,1,0:T(8,128)}), f32[2,512,512]{2,1,0:T(8,128)}) %all-gather.9.cloned.1.call-update) | async-done | bytes 2097168 | tf_op jit(solution)/shard_map/all_gather | solution.py:57
  415.4 11.7 %cholesky.358 = f32[128,128]{1,0:T(8,128)S(1)} custom-call(f32[128,128]{1,0:T(8,128)S(1)} %cholesky.439), custom_call_target="Cholesky" | custom-call | tf_op jit(solution)/shard_map/jit(cholesky)/cholesky | solution.py:16
  427.3 9.8 %custom-call.31 = f32[1,128,128]{1,2,0:T(8,128)S(1)} custom-call(f32[1,128,128]{2,1,0:T(8,128)S(1)} %get-tuple-element.49), custom_call_target="InvertDiagBlocksLowerTriangular" | custom-call | tf_op jit(solution)/shard_map/jit(cholesky)/cholesky | solution.py:16
  439.7 11.7 %cholesky.377 = f32[128,128]{1,0:T(8,128)S(1)} custom-call(f32[128,128]{1,0:T(8,128)S(1)} %cholesky.443), custom_call_target="Cholesky" | custom-call | tf_op jit(solution)/shard_map/jit(cholesky)/cholesky | solution.py:16
  451.4 10.2 %custom-call.32 = f32[1,128,128]{1,2,0:T(8,128)S(1)} custom-call(f32[1,128,128]{2,1,0:T(8,128)S(1)} %get-tuple-element.46), custom_call_target="InvertDiagBlocksLowerTriangular" | custom-call | tf_op jit(solution)/shard_map/jit(cholesky)/cholesky | solution.py:16
  463.2 11.7 %cholesky.398 = f32[128,128]{1,0:T(8,128)S(1)} custom-call(f32[128,128]{1,0:T(8,128)S(1)} %cholesky.448), custom_call_target="Cholesky" | custom-call | tf_op jit(solution)/shard_map/jit(cholesky)/cholesky | solution.py:16
  474.9 9.8 %custom-call.33 = f32[1,128,128]{1,2,0:T(8,128)S(1)} custom-call(f32[1,128,128]{2,1,0:T(8,128)S(1)} %get-tuple-element.43), custom_call_target="InvertDiagBlocksLowerTriangular" | custom-call | tf_op jit(solution)/shard_map/jit(cholesky)/cholesky | solution.py:16
  486.2 11.9 %cholesky.415 = f32[128,128]{1,0:T(8,128)S(1)} custom-call(f32[128,128]{1,0:T(8,128)S(1)} %convolution_subtract_fusion.12), custom_call_target="Cholesky" | custom-call | tf_op jit(solution)/shard_map/jit(cholesky)/cholesky | solution.py:16
  504.5 11.8 %while.5 = (s32[]{:T(128)}, f32[512,512]{1,0:T(8,128)}, s32[4,2]{0,1:T(2,128)S(1)}, f32[4,128,128]{2,1,0:T(8,128)S(1)}, s32[]{:T(128)}) while((s32[]{:T(128)}, f32[512,512]{1,0:T(8,128)}, s32[4,2]{0,1:T(2,128)S(1)}, f32[4,128,128]{2,1,0:T(8,128)S(1)}, s32[]{:T(128)}) %tuple.84), condition=%wide.while_cond.clone, body=%wide.while_body.clone.sunk | while | flops 2 | bytes 131181 | solution.py:17
  516.3 39.3 %custom-call.34 = f32[4,128,128]{1,2,0:T(8,128)S(1)} custom-call(f32[4,128,128]{2,1,0:T(8,128)S(1)} %get-tuple-element.19), custom_call_target="InvertDiagBlocksLowerTriangular" | custom-call | tf_op jit(solution)/shard_map/jit(_solve_triangular)/triangular_solve | solution.py:17
  561.4 3.1 convolution_select_fusion
  564.9 4.6 all_to_all.27
  570.9 53.2 %all-reduce.12.cloned.1.call-done = f32[1024,256]{1,0:T(8,128)} async-done(((f32[1024,256]{1,0:T(8,128)}), f32[1024,256]{1,0:T(8,128)}) %all-reduce.12.cloned.1.call-update) | async-done | bytes 1048592 | tf_op jit(solution)/shard_map/psum | solution.py:12
  624.2 53.5 %all-gather.11.cloned.1.call-done = f32[4096,256]{1,0:T(8,128)} async-done(((f32[1024,256]{1,0:T(8,128)}), f32[4096,256]{1,0:T(8,128)}) %all-gather.11.cloned.1.call-update) | async-done | bytes 4194320 | tf_op jit(solution)/shard_map/all_gather | solution.py:69
  680.2 5.2 convolution_subtract_fusion
  686.9 10.7 %reduce-scatter.8.cloned.1.call-done = f32[512,1024]{1,0:T(8,128)} async-done(((f32[1024,1024]{1,0:T(8,128)}), f32[512,1024]{1,0:T(8,128)}) %reduce-scatter.8.cloned.1.call-update) | async-done | bytes 2097168 | tf_op jit(solution)/shard_map/reduce_scatter | solution.py:79
  (145 shorter events, 79.6 us)
Async XLA Ops:
  7.2 59.7 %all-reduce.6.cloned.1.call-start = ((), (), s32[]{:S(2)}) async-start(), calls=%async_computation.5 | async-start | bytes 2097152 | tf_op jit(solution)/shard_map/psum | solution.py:12
  9.5 69.5 %all-gather.5.cloned.1.call-start = ((), (), s32[]{:S(2)}) async-start(), calls=%async_computation.6 | async-start | bytes 3145728 | tf_op jit(solution)/shard_map/all_gather | solution.py:57
  66.9 153.0 %reduce-scatter.4.cloned.1.call-start = ((), (), s32[]{:S(2)}) async-start(), calls=%async_computation.7 | async-start | bytes 3145728 | tf_op jit(solution)/shard_map/reduce_scatter | solution.py:58
  70.0 212.1 %all-reduce.8.cloned.1.call-start = ((), (), s32[]{:S(2)}) async-start(), calls=%async_computation.8 | async-start | bytes 2097152 | tf_op jit(solution)/shard_map/psum | solution.py:12
  81.4 1.0 copy-start.5
  228.9 106.8 %all-gather.7.cloned.1.call-start = ((), (), s32[]{:S(2)}) async-start(), calls=%async_computation.9 | async-start | bytes 5242880 | tf_op jit(solution)/shard_map/all_gather | solution.py:69
  282.1 55.2 %copy-start.3 = (f32[1024,256]{1,0:T(8,128)S(1)}, f32[1024,256]{1,0:T(8,128)}, u32[]{:S(2)}) copy-start(f32[1024,256]{1,0:T(8,128)} %all-reduce.8.cloned.1.call-done) | copy-start | bytes 3145732
  282.2 115.5 %all-reduce.10.cloned.1.call-start = ((), (), s32[]{:S(2)}) async-start(), calls=%async_computation.11 | async-start | bytes 2097152 | tf_op jit(solution)/shard_map/psum | solution.py:12
  335.7 2.5 copy-start.2
  342.0 1.9 copy-start
  345.0 64.8 %all-gather.9.cloned.1.call-start = ((), (), s32[]{:S(2)}) async-start(), calls=%async_computation.12 | async-start | bytes 3145728 | tf_op jit(solution)/shard_map/all_gather | solution.py:57
  397.7 163.7 %reduce-scatter.6.cloned.1.call-start = ((), (), s32[]{:S(2)}) async-start(), calls=%async_computation.10 | async-start | bytes 3145728 | tf_op jit(solution)/shard_map/reduce_scatter | solution.py:58
  400.8 223.2 %all-reduce.12.cloned.1.call-start = ((), (), s32[]{:S(2)}) async-start(), calls=%async_computation.13 | async-start | bytes 2097152 | tf_op jit(solution)/shard_map/psum | solution.py:12
  414.5 1.0 copy-start.6
  570.9 106.8 %all-gather.11.cloned.1.call-start = ((), (), s32[]{:S(2)}) async-start(), calls=%async_computation.14 | async-start | bytes 5242880 | tf_op jit(solution)/shard_map/all_gather | solution.py:69
  624.1 55.2 %copy-start.4 = (f32[1024,256]{1,0:T(8,128)S(1)}, f32[1024,256]{1,0:T(8,128)}, u32[]{:S(2)}) copy-start(f32[1024,256]{1,0:T(8,128)} %all-reduce.12.cloned.1.call-done) | copy-start | bytes 3145732
  624.1 73.5 %reduce-scatter.8.cloned.1.call-start = ((), (), s32[]{:S(2)}) async-start(), calls=%async_computation.15 | async-start | bytes 6291456 | tf_op jit(solution)/shard_map/reduce_scatter | solution.py:79
  677.6 2.5 copy-start.1
Sparse Core Ops, SparseCore 0:
  11.6 55.1 all-reduce.5
  68.4 10.5 all-gather.4
  81.8 10.9 reduce-scatter.3
  229.0 53.0 all-reduce.7
  283.8 51.8 all-gather.6
  345.2 52.4 all-reduce.9
  399.2 10.5 all-gather.8
  412.6 10.9 reduce-scatter.5
  571.0 53.0 all-reduce.11
  625.8 51.8 all-gather.10
  685.5 12.0 reduce-scatter.7
